TPU v7x, 32 devices: a 4x4x1 block of a 4x4x8 slice. The times are simulated.
32 devices in a mesh: dp: 2 (over z, core), tp: 16 (over x, y).
Axes of the slice: x: 4, y: 4, z: 1, core: 2. Of those that a mesh axis runs over, the one named last changes fastest.
The devices are a block of a 4x4x8 slice.
Arguments:
- x: bfloat16 [4096, 3072], P('dp'), parts along dimension 0
- dy: bfloat16 [4096, 3072], P('dp'), parts along dimension 0
- gate: bfloat16 [4096, 8192], P('dp', 'tp'), parts along dimension 0
- up: bfloat16 [4096, 8192], P('dp', 'tp'), parts along dimension 0
- w_gate: bfloat16 [3072, 8192], P(None, 'tp')
- w_up: bfloat16 [3072, 8192], P(None, 'tp')
- w_down: bfloat16 [8192, 3072], P('tp')
Outputs:
- output 1: bfloat16 [4096, 3072], P('dp'), parts along dimension 0
- output 2: bfloat16 [6144, 8192], P('dp', 'tp'), parts along dimension 0
- output 3: bfloat16 [6144, 8192], P('dp', 'tp'), parts along dimension 0
- output 4: bfloat16 [16384, 3072], P(('dp', 'tp')), parts along dimension 0
There are 2 independent parts. A program takes and returns all parts, laid end to end along the dimension named above; an argument that names none is the same for every part.
All inputs are finite; a program needn't handle non-finite values.
Results may differ from a plain program's by a relative error of at most 0.012.
Values are sent between devices in bfloat16 or wider.
A program may use at most 768 MiB of HBM per device.

v0:
```python
import jax
import jax.numpy as jnp
from jax import lax
from jax.sharding import PartitionSpec as P


def act(gate, up):
    return jax.nn.silu(gate) * up


def solution(mesh):
    def step(x, dy, gate, up, w_gate, w_up, w_down):
        hidden, back = jax.vjp(act, gate.astype(jnp.float32), up.astype(jnp.float32))
        d_hidden = jnp.dot(dy, w_down.T, preferred_element_type=jnp.float32)
        d_gate, d_up = (g.astype(jnp.bfloat16) for g in back(d_hidden))
        term = jnp.dot(d_gate, w_gate.T, preferred_element_type=jnp.float32) + jnp.dot(d_up, w_up.T, preferred_element_type=jnp.float32)
        dx = lax.psum(term.astype(jnp.bfloat16), "tp")
        dw_gate = jnp.dot(x.T, d_gate, preferred_element_type=jnp.float32)
        dw_up = jnp.dot(x.T, d_up, preferred_element_type=jnp.float32)
        dw_down = jnp.dot(hidden.astype(jnp.bfloat16).T, dy, preferred_element_type=jnp.float32)
        return dx, *(g.astype(jnp.bfloat16) for g in (dw_gate, dw_up, dw_down))

    tokens, columns, rows = P("dp", None), P(None, "tp"), P("tp", None)
    return jax.shard_map(
        step,
        mesh=mesh,
        in_specs=(tokens, tokens, P("dp", "tp"), P("dp", "tp"), columns, columns, rows),
        out_specs=(tokens, P("dp", "tp"), P("dp", "tp"), P(("dp", "tp"), None)),
        check_vma=False,
    )
```

profile of v0, /device:TPU:97, one launch (start us, length us, event | category | flops | bytes accessed | tf_op | source)
XLA Modules:
  0.0 243.1 jit_solution(14699166419640431458)
XLA Ops:
  7.2 0.0 copy-start
  7.2 0.1 all-reduce.2.cloned.1.call-start
  7.3 16.1 %fusion.6 = (bf16[2048,512]{1,0:T(8,128)(2,1)S(1)}, f32[2048,512]{1,0:T(8,128)}) fusion(bf16[2048,512]{1,0:T(8,128)(2,1)} %param.9, bf16[2048,512]{1,0:T(8,128)(2,1)} %param.10, bf16[2048,3072]{1,0:T(8,128)(2,1)} %param.8, bf16[512,3072]{1,0:T(8,128)(2,1)} %param.13), kind=kOutput, calls=%fused_computation.16 | convolution fusion | flops 6456082432 | bytes 26214400 | tf_op jit(solution)/shard_map/dot_general | solution.py:14
  23.3 0.0 copy-start.4
  23.3 0.0 copy-done
  23.3 0.0 copy-start.2
  23.3 0.0 copy-start.3
  23.3 12.0 %fusion.11 = f32[2048,3072]{1,0:T(8,128)} fusion(bf16[2048,512]{1,0:T(8,128)(2,1)S(1)} %get-tuple-element.8, bf16[3072,512]{1,0:T(8,128)(2,1)S(1)} %copy-done), kind=kOutput, calls=%fused_computation.21 | convolution fusion | flops 6442450944 | bytes 30408704 | tf_op jit(solution)/shard_map/dot_general | solution.py:16
  35.3 0.0 copy-done.4
  35.3 0.0 copy-done.2
  35.3 0.0 copy-done.3
  35.3 18.7 %add_convert_fusion = bf16[2048,3072]{1,0:T(8,128)(2,1)} fusion(f32[2048,3072]{1,0:T(8,128)} %fusion.11, bf16[3072,512]{1,0:T(8,128)(2,1)S(1)} %copy-done.2, f32[2048,512]{1,0:T(8,128)} %get-tuple-element.9, bf16[2048,512]{1,0:T(8,128)(2,1)S(1)} %copy-done.3), kind=kOutput, calls=%fused_computation | convolution fusion | flops 6462373888 | bytes 47185920 | tf_op jit(solution)/shard_map/dot_general | solution.py:16
  54.0 0.1 all-reduce.2.cloned.1.call-update
  54.1 10.6 %fusion.7 = bf16[3072,512]{0,1:T(8,128)(2,1)S(1)} fusion(bf16[2048,512]{1,0:T(8,128)(2,1)} %copy-done.4, bf16[2048,3072]{1,0:T(8,128)(2,1)} %param.7), kind=kOutput, calls=%fused_computation.18 | convolution fusion | flops 6444023808 | bytes 17825792 | tf_op jit(solution)/shard_map/dot_general | solution.py:18
  64.7 2.8 %copy.11 = bf16[3072,512]{1,0:T(8,128)(2,1)} copy(bf16[3072,512]{0,1:T(8,128)(2,1)S(1)} %fusion.7) | data formatting | bytes 6291456
  67.4 13.0 %fusion.8 = bf16[3072,512]{0,1:T(8,128)(2,1)S(1)} fusion(bf16[2048,3072]{1,0:T(8,128)(2,1)} %param.7, f32[2048,512]{1,0:T(8,128)} %get-tuple-element.9, bf16[2048,512]{1,0:T(8,128)(2,1)} %param.9), kind=kOutput, calls=%fused_computation.19 | convolution fusion | flops 6451363840 | bytes 22020096 | tf_op jit(solution)/shard_map/dot_general | solution.py:19
  80.5 2.8 %copy.12 = bf16[3072,512]{1,0:T(8,128)(2,1)} copy(bf16[3072,512]{0,1:T(8,128)(2,1)S(1)} %fusion.8) | data formatting | bytes 6291456
  83.3 12.6 %convolution_convert_fusion = bf16[512,3072]{1,0:T(8,128)(2,1)} fusion(bf16[2048,3072]{1,0:T(8,128)(2,1)} %param.8, bf16[2048,512]{1,0:T(8,128)(2,1)} %param.10, bf16[2048,512]{1,0:T(8,128)(2,1)} %param.9), kind=kOutput, calls=%fused_computation.7 | convolution fusion | flops 6452412416 | bytes 19922944 | tf_op jit(solution)/shard_map/dot_general | solution.py:20
  95.9 129.6 %all-reduce.2.cloned.1.call-done = bf16[2048,3072]{1,0:T(8,128)(2,1)} async-done(((bf16[2048,3072]{1,0:T(8,128)(2,1)}), bf16[2048,3072]{1,0:T(8,128)(2,1)}) %all-reduce.2.cloned.1.call-update) | async-done | bytes 12582928 | tf_op jit(solution)/shard_map/psum | solution.py:17
  225.5 0.0 copy-start.1
  225.5 10.8 %copy.14 = bf16[2048,3072]{1,0:T(8,128)(2,1)} copy(bf16[2048,3072]{1,0:T(8,128)(2,1)} %all-reduce.2.cloned.1.call-done) | data formatting | bytes 25165824
  236.3 0.0 copy-done.1
Async XLA Ops:
  7.2 16.2 %copy-start = (bf16[3072,512]{1,0:T(8,128)(2,1)S(1)}, bf16[3072,512]{1,0:T(8,128)(2,1)}, u32[]{:S(2)}) copy-start(bf16[3072,512]{1,0:T(8,128)(2,1)} %param.11) | copy-start | bytes 9437188
  7.2 218.3 %all-reduce.2.cloned.1.call-start = ((), (), s32[]{:S(2)}) async-start(), calls=%async_computation | async-start | bytes 25165824 | tf_op jit(solution)/shard_map/psum | solution.py:17
  23.3 12.0 %copy-start.4 = (bf16[2048,512]{1,0:T(8,128)(2,1)}, bf16[2048,512]{1,0:T(8,128)(2,1)S(1)}, u32[]{:S(2)}) copy-start(bf16[2048,512]{1,0:T(8,128)(2,1)S(1)} %get-tuple-element.8) | copy-start | bytes 6291460
  23.3 12.0 %copy-start.2 = (bf16[3072,512]{1,0:T(8,128)(2,1)S(1)}, bf16[3072,512]{1,0:T(8,128)(2,1)}, u32[]{:S(2)}) copy-start(bf16[3072,512]{1,0:T(8,128)(2,1)} %param.12) | copy-start | bytes 9437188
  23.3 12.0 %copy-start.3 = (bf16[2048,512]{1,0:T(8,128)(2,1)S(1)}, bf16[2048,512]{1,0:T(8,128)(2,1)}, u32[]{:S(2)}) copy-start(bf16[2048,512]{1,0:T(8,128)(2,1)} %param.9) | copy-start | bytes 6291460
  225.5 10.8 %copy-start.1 = (bf16[3072,512]{1,0:T(8,128)(2,1)S(1)}, bf16[3072,512]{1,0:T(8,128)(2,1)}, u32[]{:S(2)}) copy-start(bf16[3072,512]{1,0:T(8,128)(2,1)} %param.11) | copy-start | bytes 9437188
Sparse Core Ops, SparseCore 0:
  54.2 171.2 all-reduce.1
where the time goes:
time: 243 us
  waiting for transfers between devices  130 us (53%)
  matrix products  82.9 us (34%)
  local copies, waits for them, and re-layouts  16.4 us (7%)
  between operations  14.1 us (6%)
    psum x1, waiting for transfers between devices, step(): dx = lax.psum(term.astype(jnp.bfloat16), 'tp')  130 us
    dot_general x1, matrix products, step(): jnp.dot(d_up, w_up.T, preferred_element_type=jnp.float32)  18.7 us
    unnamed x13, local copies, waits for them, and re-layouts  16.4 us
    dot_general x1, matrix products, step(): d_hidden = jnp.dot(dy, w_down.T, preferred_element_type=jnp.float32)  16.1 us
    dot_general x1, matrix products, step(): dw_up = jnp.dot(x.T, d_up, preferred_element_type=jnp.float32)  13 us
    dot_general x1, matrix products, step(): jnp.dot(hidden.astype(jnp.bfloat16).T, dy, preferred_element_type=jnp.flo...  12.6 us
    dot_general x1, matrix products, step(): jnp.dot(d_gate, w_gate.T, preferred_element_type=jnp.float32)  12 us
    dot_general x1, matrix products, step(): dw_gate = jnp.dot(x.T, d_gate, preferred_element_type=jnp.float32)  10.6 us
  transfers between devices with their start and end apart: 1, of which 1 were waited for; matrix products, arithmetic and copies ran while one was open for 17% of the time, Pallas kernels for 0%

commit v1 on v0

v1 whole, which is shorter than its diff:
```python
import jax
import jax.numpy as jnp
from jax import lax
from jax.experimental import pallas as pl
from jax.experimental.pallas import tpu as pltpu
from jax.sharding import PartitionSpec as P

MESH = pl.DeviceIdType.MESH
F32, BF16 = jnp.float32, jnp.bfloat16
BLOCK = 256
COLS = 256
SLOTS = 4
SIDE = 4
NT = (((1,), (1,)), ((), ()))
NN = (((1,), (0,)), ((), ()))


def dot(a, b, dims):
    return lax.dot_general(a, b, dims, preferred_element_type=F32)


def kernel(
    x, dy, gate, up, w_gate, w_up, w_down,
    dx, o_gate, o_up, o_down,
    acc, acc2, major_send, major_recv, minor_send, minor_recv,
    d_gate, d_up, hidden_t, dy_in, gate_in, up_in, x_cols, dy_cols,
    w_sem, in_sem, cols_sem, rs_send_sem, rs_recv_sem, ag_send_sem, ag_recv_sem,
):
    rows, depth = x.shape
    blocks = rows // BLOCK
    big, small = BLOCK // SIDE, BLOCK // SIDE // SIDE
    half, quarter = depth // 2, depth // 4
    pieces = depth // COLS

    me = lax.axis_index("tp")
    px, py = lax.div(me, SIDE), lax.rem(me, SIDE)

    def wrap(k):
        return lax.rem(k + SIDE, SIDE)

    x_ring = [wrap(px + 1) * SIDE + py, wrap(px - 1) * SIDE + py]
    y_ring = [px * SIDE + wrap(py + 1), px * SIDE + wrap(py - 1)]
    major = [(px, x_ring), (py, y_ring)]
    minor = [(py, y_ring), (px, x_ring)]

    weights = [
        pltpu.make_async_copy(w_down, o_down, w_sem.at[0]),
        pltpu.make_async_copy(w_gate, o_gate, w_sem.at[1]),
        pltpu.make_async_copy(w_up, o_up, w_sem.at[2]),
    ]

    def inputs(b):
        slot = lax.rem(b, 2)
        here = pl.ds(pl.multiple_of(b * BLOCK, BLOCK), BLOCK)
        return [
            pltpu.make_async_copy(src.at[here], dst.at[slot], in_sem.at[slot, k])
            for k, (src, dst) in enumerate([(dy, dy_in), (gate, gate_in), (up, up_in)])
        ]

    def columns(k):
        slot = lax.rem(k, 2)
        here = pl.ds(pl.multiple_of(k * COLS, COLS), COLS)
        return [
            pltpu.make_async_copy(src.at[:, here], dst.at[slot], cols_sem.at[slot, j])
            for j, (src, dst) in enumerate([(x, x_cols), (dy, dy_cols)])
        ]

    weights[0].start()
    for c in inputs(0):
        c.start()
    weights[1].start()
    weights[2].start()

    barrier = pltpu.get_barrier_semaphore()
    for n in x_ring + y_ring:
        pl.semaphore_signal(barrier, inc=1, device_id={"tp": n}, device_id_type=MESH)
    pl.semaphore_wait(barrier, 4)

    def remote(src, dst, send, recv, to):
        return pltpu.make_async_remote_copy(
            src_ref=src, dst_ref=dst, send_sem=send, recv_sem=recv, device_id={"tp": to}, device_id_type=MESH
        )

    def rs(b, h, m, phase):
        slot = lax.rem(b, SLOTS)
        sent, got = ((major_send, major_recv), (minor_send, minor_recv))[phase]
        ring = (major, minor)[phase][h][1]
        return remote(
            sent.at[slot, h, m], got.at[slot, h, m],
            rs_send_sem.at[slot, phase, h, m], rs_recv_sem.at[slot, phase, h, m], ring[m % 2],
        )

    def place(b, h, phase, chunk, side):
        start = b * BLOCK + (chunk * big if phase == 0 else major[h][0] * big + chunk * small)
        size = big if phase == 0 else small
        return dx.at[pl.ds(pl.multiple_of(start, size), size), pl.ds(h * half + side * quarter, quarter)]

    def ag(b, h, m, phase):
        slot = lax.rem(b, SLOTS)
        at, ring = (major, minor)[phase][h]
        chunk = [at, at, at, at, wrap(at - 1), wrap(at + 1)][m]
        ref = place(b, h, phase, chunk, (0, 1, 1, 0, 0, 1)[m])
        return remote(ref, ref, ag_send_sem.at[slot, phase, h, m], ag_recv_sem.at[slot, phase, h, m], ring[m % 2])

    def source(b, h, phase, chunk, side):
        slot = lax.rem(b, SLOTS - 1)
        ref, size = ((acc, big), (acc2, small))[phase]
        return ref[slot, pl.ds(pl.multiple_of(chunk * size, size), size), pl.ds(h * half + side * quarter, quarter)]

    def scatter_first(b, phase):
        slot = lax.rem(b, SLOTS)
        sent = (major_send, minor_send)[phase]
        for h in range(2):
            at = (major, minor)[phase][h][0]
            chunks = [wrap(at + 2), wrap(at + 2), wrap(at + 1), wrap(at - 1)]
            for m in range(4):
                sent[slot, h, m] = source(b, h, phase, chunks[m], (0, 1, 1, 0)[m]).astype(BF16)
        for m in range(4):
            for h in range(2):
                rs(b, h, m, phase).start()

    def scatter_second(b, phase):
        slot = lax.rem(b, SLOTS)
        sent, got = ((major_send, major_recv), (minor_send, minor_recv))[phase]
        for h in range(2):
            at = (major, minor)[phase][h][0]
            for m in range(2):
                rs(b, h, m, phase).wait_recv()
                chunk = wrap(at + 1) if m == 0 else wrap(at - 1)
                sent[slot, h, 4 + m] = (source(b, h, phase, chunk, m) + got[slot, h, m].astype(F32)).astype(BF16)
        for h in range(2):
            for m in range(2):
                rs(b, h, 4 + m, phase).start()

    def total(b, h, phase, side):
        slot = lax.rem(b, SLOTS)
        got = (major_recv, minor_recv)[phase]
        at = (major, minor)[phase][h][0]
        parts = ((3, 4), (2, 5))[side]
        return source(b, h, phase, at, side) + got[slot, h, parts[0]].astype(F32) + got[slot, h, parts[1]].astype(F32)

    def scatter_done(b, phase):
        for h in range(2):
            for m in range(2, 6):
                rs(b, h, m, phase).wait_recv()
            for side in range(2):
                value = total(b, h, phase, side)
                if phase == 0:
                    acc2[lax.rem(b, SLOTS - 1), :, pl.ds(h * half + side * quarter, quarter)] = value
                else:
                    place(b, h, 1, minor[h][0], side)[...] = value.astype(BF16)

    def sends_done(b, make, phase):
        for h in range(2):
            for m in range(6):
                make(b, h, m, phase).wait_send()

    def gather_first(b, phase):
        for m in range(4):
            for h in range(2):
                ag(b, h, m, phase).start()

    def gather_second(b, phase):
        for h in range(2):
            for m in range(2):
                ag(b, h, m, phase).wait_recv()
                ag(b, h, 4 + m, phase).start()

    def gather_done(b, phase):
        for h in range(2):
            for m in range(2, 6):
                ag(b, h, m, phase).wait_recv()

    def term(b):
        slot, out = lax.rem(b, 2), lax.rem(b, SLOTS - 1)
        here = pl.ds(pl.multiple_of(b * BLOCK, BLOCK), BLOCK)
        for c in inputs(b):
            c.wait()

        @pl.when(b == 0)
        def _():
            weights[0].wait()

        @pl.when(b + 1 < blocks)
        def _():
            for c in inputs(b + 1):
                c.start()

        d_hidden = dot(dy_in[slot], o_down[...], NT)
        g, u = gate_in[slot].astype(F32), up_in[slot].astype(F32)
        s = jax.nn.sigmoid(g)
        silu = g * s
        dg = (d_hidden * u * (s * (1.0 + g * (1.0 - s)))).astype(BF16)
        du = (d_hidden * silu).astype(BF16)
        d_gate[here, :] = dg
        d_up[here, :] = du
        hidden_t[:, here] = (silu * u).astype(BF16).T

        @pl.when(b == 0)
        def _():
            weights[1].wait()
            weights[2].wait()

        for j in range(4):
            cut = pl.ds(j * quarter, quarter)
            acc[out, :, cut] = dot(d_gate[here, :], o_gate[cut, :], NT) + dot(d_up[here, :], o_up[cut, :], NT)

    def weight_gradients(k):
        slot = lax.rem(k, 2)
        here = pl.ds(pl.multiple_of(k * COLS, COLS), COLS)
        for c in columns(k):
            c.wait()

        @pl.when(k + 1 < pieces)
        def _():
            for c in columns(k + 1):
                c.start()

        x_t = x_cols[slot].T
        o_gate[here, :] = dot(x_t, d_gate[...], NN).astype(BF16)
        o_up[here, :] = dot(x_t, d_up[...], NN).astype(BF16)
        o_down[:, here] = dot(hidden_t[...], dy_cols[slot], NN).astype(BF16)

    per_step = 2
    first_step = blocks

    def at(i, lag, f):
        b = i - lag

        @pl.when(jnp.logical_and(b >= 0, b < blocks))
        def _():
            f(b)

    def weights_at(i, j):
        k = (i - first_step) * per_step + j

        @pl.when(jnp.logical_and(i >= first_step, k < pieces))
        def _():
            weight_gradients(k)

    def step(i, carry):
        at(i, 4, lambda b: sends_done(b, rs, 0))

        @pl.when(i < blocks)
        def _():
            term(i)
            scatter_first(i, 0)

        @pl.when(i == first_step - 1)
        def _():
            for c in columns(0):
                c.start()

        def last(b):
            gather_done(b, 0)
            sends_done(b, ag, 0)

        at(i, 8, last)
        at(i, 7, lambda b: gather_second(b, 0))

        def gather_rows(b):
            gather_done(b, 1)
            sends_done(b, ag, 1)
            gather_first(b, 0)

        at(i, 6, gather_rows)
        weights_at(i, 0)
        at(i, 5, lambda b: gather_second(b, 1))

        def finish(b):
            scatter_done(b, 1)
            gather_first(b, 1)

        at(i, 4, finish)
        at(i, 3, lambda b: scatter_second(b, 1))
        at(i, 6, lambda b: sends_done(b, rs, 1))
        weights_at(i, 1)

        def turn(b):
            scatter_done(b, 0)
            scatter_first(b, 1)

        at(i, 2, turn)
        at(i, 1, lambda b: scatter_second(b, 0))
        return carry

    lax.fori_loop(0, blocks + 8, step, 0)


def write_out(dx, a, b, c, o_dx, o_a, o_b, o_c, sem):
    copies = []
    for src, dst in ((dx, o_dx), (a, o_a), (b, o_b), (c, o_c)):
        n = src.shape[0] // 4
        for j in range(4):
            cut = pl.ds(j * n, n)
            copies.append(pltpu.make_async_copy(src.at[cut], dst.at[cut], sem.at[len(copies)]))
    for c in copies:
        c.start()
    for c in copies:
        c.wait()


def solution(mesh):
    assert mesh.shape["tp"] == SIDE * SIDE

    def step(x, dy, gate, up, w_gate, w_up, w_down):
        rows, depth = x.shape
        units = gate.shape[1]
        big, small, quarter = BLOCK // SIDE, BLOCK // SIDE // SIDE, depth // 4
        outs = [x, w_gate, w_up, w_down]
        dma = pltpu.SemaphoreType.DMA
        flops = 2 * 6 * rows * depth * units
        result = pl.pallas_call(
            kernel,
            out_shape=[pltpu.VMEM(o.shape, BF16) for o in outs],
            in_specs=[pl.BlockSpec(memory_space=pltpu.HBM)] * 7,
            out_specs=[pl.BlockSpec(memory_space=pltpu.VMEM)] * 4,
            scratch_shapes=[
                pltpu.VMEM((SLOTS - 1, BLOCK, depth), F32),
                pltpu.VMEM((SLOTS - 1, big, depth), F32),
                pltpu.VMEM((SLOTS, 2, 6, big, quarter), BF16),
                pltpu.VMEM((SLOTS, 2, 6, big, quarter), BF16),
                pltpu.VMEM((SLOTS, 2, 6, small, quarter), BF16),
                pltpu.VMEM((SLOTS, 2, 6, small, quarter), BF16),
                pltpu.VMEM((rows, units), BF16),
                pltpu.VMEM((rows, units), BF16),
                pltpu.VMEM((units, rows), BF16),
                pltpu.VMEM((2, BLOCK, depth), BF16),
                pltpu.VMEM((2, BLOCK, units), BF16),
                pltpu.VMEM((2, BLOCK, units), BF16),
                pltpu.VMEM((2, rows, COLS), BF16),
                pltpu.VMEM((2, rows, COLS), BF16),
                dma((3,)),
                dma((2, 3)),
                dma((2, 2)),
                dma((SLOTS, 2, 2, 6)),
                dma((SLOTS, 2, 2, 6)),
                dma((SLOTS, 2, 2, 6)),
                dma((SLOTS, 2, 2, 6)),
            ],
            compiler_params=pltpu.CompilerParams(
                collective_id=0, has_side_effects=True, vmem_limit_bytes=42 * 2**20
            ),
            cost_estimate=pl.CostEstimate(flops=flops, bytes_accessed=60 * 2**20, transcendentals=rows * units),
        )(x, dy, gate, up, w_gate, w_up, w_down)
        return pl.pallas_call(
            write_out,
            out_shape=[pltpu.HBM(o.shape, BF16) for o in outs],
            in_specs=[pl.BlockSpec(memory_space=pltpu.VMEM)] * 4,
            out_specs=[pl.BlockSpec(memory_space=pltpu.HBM)] * 4,
            scratch_shapes=[dma((16,))],
            compiler_params=pltpu.CompilerParams(has_side_effects=True, vmem_limit_bytes=2**20),
        )(*result)

    tokens, columns, rows = P("dp", None), P(None, "tp"), P("tp", None)
    return jax.shard_map(
        step,
        mesh=mesh,
        in_specs=(tokens, tokens, P("dp", "tp"), P("dp", "tp"), columns, columns, rows),
        out_specs=(tokens, P("dp", "tp"), P("dp", "tp"), P(("dp", "tp"), None)),
        check_vma=False,
    )
```

time: 243 us -> 152 us (0.63)
  Pallas kernels: 0 us -> 151 us
  waiting for transfers between devices: 130 us -> 0 us
  matrix products: 82.9 us -> 0 us
  local copies, waits for them, and re-layouts: 16.4 us -> 0 us
  between operations: 14.1 us -> 0.64 us
    pallas_call x0 -> x2, Pallas kernels: none -> 151 us  [the longest x1 143 us: step(): pl.pallas_call(kernel, out_shape=[pltpu.VMEM(o.shape, BF16) for o in outs...]
    psum x1 -> x0, waiting for transfers between devices: 130 us -> none  [step(): dx = lax.psum(term.astype(jnp.bfloat16), 'tp')]
    dot_general x6 -> x0, matrix products: 82.9 us -> none  [the longest x1 18.7 us: step(): jnp.dot(d_up, w_up.T, preferred_element_type=jnp.float32)]
    unnamed x13 -> x0, local copies, waits for them, and re-layouts: 16.4 us -> none
  transfers between devices with their start and end apart: 1 -> 0, of which waited for: 1 -> 0; matrix products, arithmetic and copies ran while one was open for 17% -> 0% of each run, Pallas kernels for 0% -> 0%
where the time goes in v1:
time: 152 us
  Pallas kernels  151 us (99%)
    pallas_call x1, Pallas kernels, step(): pl.pallas_call(kernel, out_shape=[pltpu.VMEM(o.shape, BF16) for o in outs...  143 us
    pallas_call x1, Pallas kernels, step(): pl.pallas_call(write_out, out_shape=[pltpu.HBM(o.shape, BF16) for o in ou...  7.59 us

profile of v1, /device:TPU:97, one launch (start us, length us, event | category | flops | bytes accessed | tf_op | source)
XLA Modules:
  0.0 151.6 jit_solution(4436551871774570127)
XLA Ops:
  0.6 143.3 %shard_map.102 = (bf16[2048,3072]{1,0:T(8,128)(2,1)S(1)}, bf16[3072,512]{1,0:T(8,128)(2,1)S(1)}, bf16[3072,512]{1,0:T(8,128)(2,1)S(1)}, bf16[512,3072]{1,0:T(8,128)(2,1)S(1)}) custom-call(bf16[2048,3072]{1,0:T(8,128)(2,1)} %x.1, bf16[2048,3072]{1,0:T(8,128)(2,1)} %dy.1, bf16[2048,512]{1,0:T(8,128)(2,1)} %gate.1, bf16[2048,512]{1,0:T(8,128)(2,1)} %up.1, ...), custom_call_target="tpu_custom_call" | custom-call | flops 38654705664 | bytes 62914560 | tf_op jit(solution)/shard_map/pallas_call | solution.py:313
  144.0 7.6 %shard_map.103 = (bf16[2048,3072]{1,0:T(8,128)(2,1)}, bf16[3072,512]{1,0:T(8,128)(2,1)}, bf16[3072,512]{1,0:T(8,128)(2,1)}, bf16[512,3072]{1,0:T(8,128)(2,1)}) custom-call(bf16[2048,3072]{1,0:T(8,128)(2,1)S(1)} %get-tuple-element.8.dx, bf16[3072,512]{1,0:T(8,128)(2,1)S(1)} %get-tuple-element.9.a, bf16[3072,512]{1,0:T(8,128)(2,1)S(1)} %get-tuple-element.10.b, ...), custom_call_target="tpu_custom_call" | custom-call | tf_op jit(solution)/shard_map/pallas_call | solution.py:346

commit v2 on v1

--- a/solution.py
+++ b/solution.py
@@ -11,6 +11,7 @@
 COLS = 256
 SLOTS = 4
 SIDE = 4
+ORDER = (0, 2, 1, 3)
 NT = (((1,), (1,)), ((), ()))
 NN = (((1,), (0,)), ((), ()))
 
@@ -43,10 +44,11 @@
     major = [(px, x_ring), (py, y_ring)]
     minor = [(py, y_ring), (px, x_ring)]
 
-    weights = [
-        pltpu.make_async_copy(w_down, o_down, w_sem.at[0]),
-        pltpu.make_async_copy(w_gate, o_gate, w_sem.at[1]),
-        pltpu.make_async_copy(w_up, o_up, w_sem.at[2]),
+    quarters = [pl.ds(j * quarter, quarter) for j in range(4)]
+    down_in = [pltpu.make_async_copy(w_down.at[:, c], o_down.at[:, c], w_sem.at[0, j]) for j, c in enumerate(quarters)]
+    gate_up_in = [
+        [pltpu.make_async_copy(src.at[c], dst.at[c], w_sem.at[k, j]) for k, (src, dst) in enumerate([(w_gate, o_gate), (w_up, o_up)], 1)]
+        for j, c in enumerate(quarters)
     ]
 
     def inputs(b):
@@ -54,7 +56,15 @@
         here = pl.ds(pl.multiple_of(b * BLOCK, BLOCK), BLOCK)
         return [
             pltpu.make_async_copy(src.at[here], dst.at[slot], in_sem.at[slot, k])
-            for k, (src, dst) in enumerate([(dy, dy_in), (gate, gate_in), (up, up_in)])
+            for k, (src, dst) in enumerate([(gate, gate_in), (up, up_in)])
+        ]
+
+    def dy_block(b):
+        slot = lax.rem(b, 2)
+        here = pl.ds(pl.multiple_of(b * BLOCK, BLOCK), BLOCK)
+        return [
+            pltpu.make_async_copy(dy.at[here, c], dy_in.at[slot, :, c], in_sem.at[slot, 2 + j])
+            for j, c in enumerate(quarters)
         ]
 
     def columns(k):
@@ -65,16 +75,18 @@
             for j, (src, dst) in enumerate([(x, x_cols), (dy, dy_cols)])
         ]
 
-    weights[0].start()
     for c in inputs(0):
         c.start()
-    weights[1].start()
-    weights[2].start()
+    for pair in zip(down_in, dy_block(0)):
+        for c in pair:
+            c.start()
+    for j in ORDER:
+        for c in gate_up_in[j]:
+            c.start()
 
     barrier = pltpu.get_barrier_semaphore()
     for n in x_ring + y_ring:
         pl.semaphore_signal(barrier, inc=1, device_id={"tp": n}, device_id_type=MESH)
-    pl.semaphore_wait(barrier, 4)
 
     def remote(src, dst, send, recv, to):
         return pltpu.make_async_remote_copy(
@@ -87,8 +99,28 @@
         ring = (major, minor)[phase][h][1]
         return remote(
             sent.at[slot, h, m], got.at[slot, h, m],
-            rs_send_sem.at[slot, phase, h, m], rs_recv_sem.at[slot, phase, h, m], ring[m % 2],
+            rs_send_sem.at[slot, phase], rs_recv_sem.at[slot, phase, int(m >= 2)], ring[m % 2],
         )
+
+    def taken(ref, sem):
+        pltpu.make_async_copy(ref, ref, sem).wait()
+
+    def rs_got(b, phase, late):
+        slot = lax.rem(b, SLOTS)
+        got = (major_recv, minor_recv)[phase]
+        taken(got.at[slot, :, pl.ds(2, 4) if late else pl.ds(0, 2)], rs_recv_sem.at[slot, phase, late])
+
+    def rs_left(b, phase):
+        slot = lax.rem(b, SLOTS)
+        taken((major_send, minor_send)[phase].at[slot], rs_send_sem.at[slot, phase])
+
+    def ag_left(b, phase):
+        slot = lax.rem(b, SLOTS)
+        taken((major_send, minor_send)[phase].at[slot], ag_send_sem.at[slot, phase])
+
+    def ag_got(b, phase):
+        slot = lax.rem(b, SLOTS)
+        taken((major_recv, minor_recv)[phase].at[slot, :, pl.ds(2, 4)], ag_recv_sem.at[slot, phase, 4])
 
     def place(b, h, phase, chunk, side):
         start = b * BLOCK + (chunk * big if phase == 0 else major[h][0] * big + chunk * small)
@@ -100,32 +132,32 @@
         at, ring = (major, minor)[phase][h]
         chunk = [at, at, at, at, wrap(at - 1), wrap(at + 1)][m]
         ref = place(b, h, phase, chunk, (0, 1, 1, 0, 0, 1)[m])
-        return remote(ref, ref, ag_send_sem.at[slot, phase, h, m], ag_recv_sem.at[slot, phase, h, m], ring[m % 2])
+        return remote(ref, ref, ag_send_sem.at[slot, phase], ag_recv_sem.at[slot, phase, 2 * h + m if m < 2 else 4], ring[m % 2])
 
     def source(b, h, phase, chunk, side):
         slot = lax.rem(b, SLOTS - 1)
         ref, size = ((acc, big), (acc2, small))[phase]
         return ref[slot, pl.ds(pl.multiple_of(chunk * size, size), size), pl.ds(h * half + side * quarter, quarter)]
 
-    def scatter_first(b, phase):
+    def scatter_first(b, phase, hs=(0, 1), ms=(0, 1, 2, 3)):
         slot = lax.rem(b, SLOTS)
         sent = (major_send, minor_send)[phase]
-        for h in range(2):
+        for h in hs:
             at = (major, minor)[phase][h][0]
             chunks = [wrap(at + 2), wrap(at + 2), wrap(at + 1), wrap(at - 1)]
-            for m in range(4):
+            for m in ms:
                 sent[slot, h, m] = source(b, h, phase, chunks[m], (0, 1, 1, 0)[m]).astype(BF16)
-        for m in range(4):
-            for h in range(2):
+        for m in ms:
+            for h in hs:
                 rs(b, h, m, phase).start()
 
     def scatter_second(b, phase):
         slot = lax.rem(b, SLOTS)
         sent, got = ((major_send, major_recv), (minor_send, minor_recv))[phase]
+        rs_got(b, phase, 0)
         for h in range(2):
             at = (major, minor)[phase][h][0]
             for m in range(2):
-                rs(b, h, m, phase).wait_recv()
                 chunk = wrap(at + 1) if m == 0 else wrap(at - 1)
                 sent[slot, h, 4 + m] = (source(b, h, phase, chunk, m) + got[slot, h, m].astype(F32)).astype(BF16)
         for h in range(2):
@@ -140,9 +172,8 @@
         return source(b, h, phase, at, side) + got[slot, h, parts[0]].astype(F32) + got[slot, h, parts[1]].astype(F32)
 
     def scatter_done(b, phase):
+        rs_got(b, phase, 1)
         for h in range(2):
-            for m in range(2, 6):
-                rs(b, h, m, phase).wait_recv()
             for side in range(2):
                 value = total(b, h, phase, side)
                 if phase == 0:
@@ -150,11 +181,6 @@
                 else:
                     place(b, h, 1, minor[h][0], side)[...] = value.astype(BF16)
 
-    def sends_done(b, make, phase):
-        for h in range(2):
-            for m in range(6):
-                make(b, h, m, phase).wait_send()
-
     def gather_first(b, phase):
         for m in range(4):
             for h in range(2):
@@ -166,44 +192,48 @@
                 ag(b, h, m, phase).wait_recv()
                 ag(b, h, 4 + m, phase).start()
 
-    def gather_done(b, phase):
-        for h in range(2):
-            for m in range(2, 6):
-                ag(b, h, m, phase).wait_recv()
-
     def term(b):
         slot, out = lax.rem(b, 2), lax.rem(b, SLOTS - 1)
         here = pl.ds(pl.multiple_of(b * BLOCK, BLOCK), BLOCK)
         for c in inputs(b):
             c.wait()
-
-        @pl.when(b == 0)
-        def _():
-            weights[0].wait()
-
-        @pl.when(b + 1 < blocks)
-        def _():
-            for c in inputs(b + 1):
-                c.start()
-
-        d_hidden = dot(dy_in[slot], o_down[...], NT)
         g, u = gate_in[slot].astype(F32), up_in[slot].astype(F32)
         s = jax.nn.sigmoid(g)
         silu = g * s
-        dg = (d_hidden * u * (s * (1.0 + g * (1.0 - s)))).astype(BF16)
-        du = (d_hidden * silu).astype(BF16)
-        d_gate[here, :] = dg
-        d_up[here, :] = du
+        slope = s * (1.0 + g * (1.0 - s))
         hidden_t[:, here] = (silu * u).astype(BF16).T
+        d_hidden = None
+        for j, c in enumerate(dy_block(b)):
+            c.wait()
+
+            @pl.when(b == 0)
+            def _(j=j):
+                down_in[j].wait()
+
+            part = dot(dy_in[slot, :, quarters[j]], o_down[:, quarters[j]], NT)
+            d_hidden = part if d_hidden is None else d_hidden + part
+        d_gate[here, :] = (d_hidden * u * slope).astype(BF16)
+        d_up[here, :] = (d_hidden * silu).astype(BF16)
+
+        @pl.when(b + 1 < blocks)
+        def _():
+            for c in dy_block(b + 1) + inputs(b + 1):
+                c.start()
 
         @pl.when(b == 0)
         def _():
-            weights[1].wait()
-            weights[2].wait()
-
-        for j in range(4):
-            cut = pl.ds(j * quarter, quarter)
+            pl.semaphore_wait(barrier, 4)
+
+        for j in ORDER:
+
+            @pl.when(b == 0)
+            def _(j=j):
+                for c in gate_up_in[j]:
+                    c.wait()
+
+            cut = quarters[j]
             acc[out, :, cut] = dot(d_gate[here, :], o_gate[cut, :], NT) + dot(d_up[here, :], o_up[cut, :], NT)
+            scatter_first(b, 0, (j // 2,), ((0, 3), (1, 2))[j % 2])
 
     def weight_gradients(k):
         slot = lax.rem(k, 2)
@@ -239,49 +269,48 @@
             weight_gradients(k)
 
     def step(i, carry):
-        at(i, 4, lambda b: sends_done(b, rs, 0))
+        at(i, 4, lambda b: rs_left(b, 0))
 
         @pl.when(i < blocks)
         def _():
             term(i)
-            scatter_first(i, 0)
 
         @pl.when(i == first_step - 1)
         def _():
             for c in columns(0):
                 c.start()
 
-        def last(b):
-            gather_done(b, 0)
-            sends_done(b, ag, 0)
-
-        at(i, 8, last)
-        at(i, 7, lambda b: gather_second(b, 0))
-
-        def gather_rows(b):
-            gather_done(b, 1)
-            sends_done(b, ag, 1)
-            gather_first(b, 0)
-
-        at(i, 6, gather_rows)
-        weights_at(i, 0)
-        at(i, 5, lambda b: gather_second(b, 1))
+        def turn(b):
+            scatter_done(b, 0)
+            scatter_first(b, 1)
+
+        at(i, 6, lambda b: rs_left(b, 1))
+        at(i, 2, turn)
+        at(i, 1, lambda b: scatter_second(b, 0))
 
         def finish(b):
             scatter_done(b, 1)
             gather_first(b, 1)
 
+        at(i, 8, lambda b: ag_left(b, 1))
         at(i, 4, finish)
         at(i, 3, lambda b: scatter_second(b, 1))
-        at(i, 6, lambda b: sends_done(b, rs, 1))
+        weights_at(i, 0)
+        at(i, 5, lambda b: gather_second(b, 1))
+        at(i, 7, lambda b: gather_second(b, 0))
+
+        def gather_rows(b):
+            ag_got(b, 1)
+            gather_first(b, 0)
+
+        at(i, 6, gather_rows)
         weights_at(i, 1)
 
-        def turn(b):
-            scatter_done(b, 0)
-            scatter_first(b, 1)
-
-        at(i, 2, turn)
-        at(i, 1, lambda b: scatter_second(b, 0))
+        def last(b):
+            ag_got(b, 0)
+            ag_left(b, 0)
+
+        at(i, 8, last)
         return carry
 
     lax.fori_loop(0, blocks + 8, step, 0)
@@ -330,13 +359,13 @@
                 pltpu.VMEM((2, BLOCK, units), BF16),
                 pltpu.VMEM((2, rows, COLS), BF16),
                 pltpu.VMEM((2, rows, COLS), BF16),
-                dma((3,)),
-                dma((2, 3)),
+                dma((3, 4)),
+                dma((2, 6)),
                 dma((2, 2)),
-                dma((SLOTS, 2, 2, 6)),
-                dma((SLOTS, 2, 2, 6)),
-                dma((SLOTS, 2, 2, 6)),
-                dma((SLOTS, 2, 2, 6)),
+                dma((SLOTS, 2)),
+                dma((SLOTS, 2, 2)),
+                dma((SLOTS, 2)),
+                dma((SLOTS, 2, 5)),
             ],
             compiler_params=pltpu.CompilerParams(
                 collective_id=0, has_side_effects=True, vmem_limit_bytes=42 * 2**20

time: 152 us -> 149 us (0.980)
  Pallas kernels: 151 us -> 148 us
    pallas_call x1, Pallas kernels: 143 us -> 140 us  [step(): pl.pallas_call(kernel, out_shape=[pltpu.VMEM(o.shape, BF16) for o in outs...]
where the time goes in v2:
time: 149 us; the launch traced here: 148 us
  Pallas kernels  148 us (99%)
    pallas_call x1, Pallas kernels, step(): pl.pallas_call(kernel, out_shape=[pltpu.VMEM(o.shape, BF16) for o in outs...  140 us
    pallas_call x1, Pallas kernels, step(): pl.pallas_call(write_out, out_shape=[pltpu.HBM(o.shape, BF16) for o in ou...  7.59 us

profile of v2, /device:TPU:97, one launch (start us, length us, event | category | flops | bytes accessed | tf_op | source)
XLA Modules:
  0.0 148.4 jit_solution(10131516645536565050)
XLA Ops:
  0.6 140.1 %shard_map.102 = (bf16[2048,3072]{1,0:T(8,128)(2,1)S(1)}, bf16[3072,512]{1,0:T(8,128)(2,1)S(1)}, bf16[3072,512]{1,0:T(8,128)(2,1)S(1)}, bf16[512,3072]{1,0:T(8,128)(2,1)S(1)}) custom-call(bf16[2048,3072]{1,0:T(8,128)(2,1)} %x.1, bf16[2048,3072]{1,0:T(8,128)(2,1)} %dy.1, bf16[2048,512]{1,0:T(8,128)(2,1)} %gate.1, bf16[2048,512]{1,0:T(8,128)(2,1)} %up.1, ...), custom_call_target="tpu_custom_call" | custom-call | flops 38654705664 | bytes 62914560 | tf_op jit(solution)/shard_map/pallas_call | solution.py:342
  140.8 7.6 %shard_map.103 = (bf16[2048,3072]{1,0:T(8,128)(2,1)}, bf16[3072,512]{1,0:T(8,128)(2,1)}, bf16[3072,512]{1,0:T(8,128)(2,1)}, bf16[512,3072]{1,0:T(8,128)(2,1)}) custom-call(bf16[2048,3072]{1,0:T(8,128)(2,1)S(1)} %get-tuple-element.8.dx, bf16[3072,512]{1,0:T(8,128)(2,1)S(1)} %get-tuple-element.9.a, bf16[3072,512]{1,0:T(8,128)(2,1)S(1)} %get-tuple-element.10.b, ...), custom_call_target="tpu_custom_call" | custom-call | tf_op jit(solution)/shard_map/pallas_call | solution.py:375

commit v3 on v2

--- a/solution.py
+++ b/solution.py
@@ -25,13 +25,14 @@
     dx, o_gate, o_up, o_down,
     acc, acc2, major_send, major_recv, minor_send, minor_recv,
     d_gate, d_up, hidden_t, dy_in, gate_in, up_in, x_cols, dy_cols,
-    w_sem, in_sem, cols_sem, rs_send_sem, rs_recv_sem, ag_send_sem, ag_recv_sem,
+    first_sem, w_sem, in_sem, cols_sem, rs_send_sem, rs_recv_sem, ag_send_sem, ag_major_sem, ag_minor_sem,
 ):
     rows, depth = x.shape
     blocks = rows // BLOCK
     big, small = BLOCK // SIDE, BLOCK // SIDE // SIDE
     half, quarter = depth // 2, depth // 4
     pieces = depth // COLS
+    units = gate.shape[1]
 
     me = lax.axis_index("tp")
     px, py = lax.div(me, SIDE), lax.rem(me, SIDE)
@@ -44,45 +45,36 @@
     major = [(px, x_ring), (py, y_ring)]
     minor = [(py, y_ring), (px, x_ring)]
 
+    def taken(ref, sem):
+        pltpu.make_async_copy(ref, ref, sem).wait()
+
+    def taken_rows(n, sem):
+        taken(d_gate.at[pl.ds(0, n)], sem)
+
     quarters = [pl.ds(j * quarter, quarter) for j in range(4)]
-    down_in = [pltpu.make_async_copy(w_down.at[:, c], o_down.at[:, c], w_sem.at[0, j]) for j, c in enumerate(quarters)]
-    gate_up_in = [
-        [pltpu.make_async_copy(src.at[c], dst.at[c], w_sem.at[k, j]) for k, (src, dst) in enumerate([(w_gate, o_gate), (w_up, o_up)], 1)]
-        for j, c in enumerate(quarters)
-    ]
+
+    def weight_quarter(j):
+        c = quarters[j]
+        for src, dst in ((w_gate, o_gate), (w_up, o_up)):
+            pltpu.make_async_copy(src.at[c], dst.at[c], w_sem.at[j]).start()
 
     def inputs(b):
         slot = lax.rem(b, 2)
         here = pl.ds(pl.multiple_of(b * BLOCK, BLOCK), BLOCK)
-        return [
-            pltpu.make_async_copy(src.at[here], dst.at[slot], in_sem.at[slot, k])
-            for k, (src, dst) in enumerate([(gate, gate_in), (up, up_in)])
-        ]
-
-    def dy_block(b):
-        slot = lax.rem(b, 2)
-        here = pl.ds(pl.multiple_of(b * BLOCK, BLOCK), BLOCK)
-        return [
-            pltpu.make_async_copy(dy.at[here, c], dy_in.at[slot, :, c], in_sem.at[slot, 2 + j])
-            for j, c in enumerate(quarters)
-        ]
+        for src, dst in ((dy, dy_in), (gate, gate_in), (up, up_in)):
+            pltpu.make_async_copy(src.at[here], dst.at[slot], in_sem.at[slot]).start()
 
     def columns(k):
         slot = lax.rem(k, 2)
         here = pl.ds(pl.multiple_of(k * COLS, COLS), COLS)
-        return [
-            pltpu.make_async_copy(src.at[:, here], dst.at[slot], cols_sem.at[slot, j])
-            for j, (src, dst) in enumerate([(x, x_cols), (dy, dy_cols)])
-        ]
-
-    for c in inputs(0):
-        c.start()
-    for pair in zip(down_in, dy_block(0)):
-        for c in pair:
-            c.start()
-    for j in ORDER:
-        for c in gate_up_in[j]:
-            c.start()
+        for src, dst in ((x, x_cols), (dy, dy_cols)):
+            pltpu.make_async_copy(src.at[:, here], dst.at[slot], cols_sem.at[slot]).start()
+
+    for src, dst in ((gate, gate_in), (up, up_in)):
+        pltpu.make_async_copy(src.at[pl.ds(0, BLOCK)], dst.at[0], first_sem.at[4]).start()
+    for j, c in enumerate(quarters):
+        pltpu.make_async_copy(w_down.at[:, c], o_down.at[:, c], first_sem.at[j]).start()
+        pltpu.make_async_copy(dy.at[pl.ds(0, BLOCK), c], dy_in.at[0, :, c], first_sem.at[j]).start()
 
     barrier = pltpu.get_barrier_semaphore()
     for n in x_ring + y_ring:
@@ -102,9 +94,6 @@
             rs_send_sem.at[slot, phase], rs_recv_sem.at[slot, phase, int(m >= 2)], ring[m % 2],
         )
 
-    def taken(ref, sem):
-        pltpu.make_async_copy(ref, ref, sem).wait()
-
     def rs_got(b, phase, late):
         slot = lax.rem(b, SLOTS)
         got = (major_recv, minor_recv)[phase]
@@ -118,9 +107,13 @@
         slot = lax.rem(b, SLOTS)
         taken((major_send, minor_send)[phase].at[slot], ag_send_sem.at[slot, phase])
 
+    def ag_sem(b, h, m, phase):
+        if phase == 0:
+            return ag_major_sem.at[lax.rem(b, SLOTS + 1), h if m < 2 else 2]
+        return ag_minor_sem.at[lax.rem(b, SLOTS), int(m >= 2)]
+
     def ag_got(b, phase):
-        slot = lax.rem(b, SLOTS)
-        taken((major_recv, minor_recv)[phase].at[slot, :, pl.ds(2, 4)], ag_recv_sem.at[slot, phase, 4])
+        taken((major_recv, minor_recv)[phase].at[lax.rem(b, SLOTS), :, pl.ds(2, 4)], ag_sem(b, 0, 2, phase))
 
     def place(b, h, phase, chunk, side):
         start = b * BLOCK + (chunk * big if phase == 0 else major[h][0] * big + chunk * small)
@@ -132,7 +125,7 @@
         at, ring = (major, minor)[phase][h]
         chunk = [at, at, at, at, wrap(at - 1), wrap(at + 1)][m]
         ref = place(b, h, phase, chunk, (0, 1, 1, 0, 0, 1)[m])
-        return remote(ref, ref, ag_send_sem.at[slot, phase], ag_recv_sem.at[slot, phase, 2 * h + m if m < 2 else 4], ring[m % 2])
+        return remote(ref, ref, ag_send_sem.at[slot, phase], ag_sem(b, h, m, phase), ring[m % 2])
 
     def source(b, h, phase, chunk, side):
         slot = lax.rem(b, SLOTS - 1)
@@ -187,38 +180,49 @@
                 ag(b, h, m, phase).start()
 
     def gather_second(b, phase):
+        if phase == 1:
+            taken(minor_recv.at[lax.rem(b, SLOTS), :, pl.ds(0, 2)], ag_sem(b, 0, 0, 1))
         for h in range(2):
+            if phase == 0:
+                taken(major_recv.at[lax.rem(b, SLOTS), 0, pl.ds(0, 2)], ag_sem(b, h, 0, 0))
             for m in range(2):
-                ag(b, h, m, phase).wait_recv()
                 ag(b, h, 4 + m, phase).start()
+
+    def activation(slot, rows):
+        g, u = gate_in[slot, rows].astype(F32), up_in[slot, rows].astype(F32)
+        s = jax.nn.sigmoid(g)
+        silu = g * s
+        return u, silu, s * (1.0 + g * (1.0 - s)), (silu * u).astype(BF16)
 
     def term(b):
         slot, out = lax.rem(b, 2), lax.rem(b, SLOTS - 1)
         here = pl.ds(pl.multiple_of(b * BLOCK, BLOCK), BLOCK)
-        for c in inputs(b):
-            c.wait()
-        g, u = gate_in[slot].astype(F32), up_in[slot].astype(F32)
-        s = jax.nn.sigmoid(g)
-        silu = g * s
-        slope = s * (1.0 + g * (1.0 - s))
-        hidden_t[:, here] = (silu * u).astype(BF16).T
+
+        @pl.when(b == 0)
+        def _():
+            taken_rows(2 * BLOCK, first_sem.at[4])
+
+        @pl.when(b > 0)
+        def _():
+            taken_rows(BLOCK * (depth + 2 * units) // units, in_sem.at[slot])
+
+        u, silu, slope, hidden = activation(slot, pl.ds(0, BLOCK))
+        hidden_t[:, here] = hidden.T
         d_hidden = None
-        for j, c in enumerate(dy_block(b)):
-            c.wait()
+        for j, c in enumerate(quarters):
 
             @pl.when(b == 0)
             def _(j=j):
-                down_in[j].wait()
-
-            part = dot(dy_in[slot, :, quarters[j]], o_down[:, quarters[j]], NT)
-            d_hidden = part if d_hidden is None else d_hidden + part
+                taken_rows((units + BLOCK) * quarter // units, first_sem.at[j])
+                if j == 0:
+                    for k in ORDER:
+                        weight_quarter(k)
+
+            piece = dot(dy_in[slot, :, c], o_down[:, c], NT)
+            d_hidden = piece if d_hidden is None else d_hidden + piece
         d_gate[here, :] = (d_hidden * u * slope).astype(BF16)
         d_up[here, :] = (d_hidden * silu).astype(BF16)
-
-        @pl.when(b + 1 < blocks)
-        def _():
-            for c in dy_block(b + 1) + inputs(b + 1):
-                c.start()
+        pl.when(b + 1 < blocks)(lambda: inputs(b + 1))
 
         @pl.when(b == 0)
         def _():
@@ -228,8 +232,7 @@
 
             @pl.when(b == 0)
             def _(j=j):
-                for c in gate_up_in[j]:
-                    c.wait()
+                taken_rows(2 * quarter, w_sem.at[j])
 
             cut = quarters[j]
             acc[out, :, cut] = dot(d_gate[here, :], o_gate[cut, :], NT) + dot(d_up[here, :], o_up[cut, :], NT)
@@ -238,13 +241,8 @@
     def weight_gradients(k):
         slot = lax.rem(k, 2)
         here = pl.ds(pl.multiple_of(k * COLS, COLS), COLS)
-        for c in columns(k):
-            c.wait()
-
-        @pl.when(k + 1 < pieces)
-        def _():
-            for c in columns(k + 1):
-                c.start()
+        taken_rows(2 * rows * COLS // units, cols_sem.at[slot])
+        pl.when(k + 1 < pieces)(lambda: columns(k + 1))
 
         x_t = x_cols[slot].T
         o_gate[here, :] = dot(x_t, d_gate[...], NN).astype(BF16)
@@ -271,14 +269,8 @@
     def step(i, carry):
         at(i, 4, lambda b: rs_left(b, 0))
 
-        @pl.when(i < blocks)
-        def _():
-            term(i)
-
-        @pl.when(i == first_step - 1)
-        def _():
-            for c in columns(0):
-                c.start()
+        pl.when(i < blocks)(lambda: term(i))
+        pl.when(i == first_step - 1)(lambda: columns(0))
 
         def turn(b):
             scatter_done(b, 0)
@@ -297,13 +289,13 @@
         at(i, 3, lambda b: scatter_second(b, 1))
         weights_at(i, 0)
         at(i, 5, lambda b: gather_second(b, 1))
-        at(i, 7, lambda b: gather_second(b, 0))
-
         def gather_rows(b):
             ag_got(b, 1)
             gather_first(b, 0)
 
         at(i, 6, gather_rows)
+        at(i, 7, lambda b: gather_second(b, 0))
+
         weights_at(i, 1)
 
         def last(b):
@@ -359,13 +351,15 @@
                 pltpu.VMEM((2, BLOCK, units), BF16),
                 pltpu.VMEM((2, rows, COLS), BF16),
                 pltpu.VMEM((2, rows, COLS), BF16),
-                dma((3, 4)),
-                dma((2, 6)),
-                dma((2, 2)),
+                dma((5,)),
+                dma((4,)),
+                dma((2,)),
+                dma((2,)),
                 dma((SLOTS, 2)),
                 dma((SLOTS, 2, 2)),
                 dma((SLOTS, 2)),
-                dma((SLOTS, 2, 5)),
+                dma((SLOTS + 1, 3)),
+                dma((SLOTS, 2)),
             ],
             compiler_params=pltpu.CompilerParams(
                 collective_id=0, has_side_effects=True, vmem_limit_bytes=42 * 2**20

time: 149 us -> 146 us (0.980)
  Pallas kernels: 148 us -> 146 us
    pallas_call x1, Pallas kernels: 140 us -> 138 us  [step(): pl.pallas_call(kernel, out_shape=[pltpu.VMEM(o.shape, BF16) for o in outs...]
where the time goes in v3:
time: 146 us
  Pallas kernels  146 us (100%)
    pallas_call x1, Pallas kernels, step(): pl.pallas_call(kernel, out_shape=[pltpu.VMEM(o.shape, BF16) for o in outs...  138 us
    pallas_call x1, Pallas kernels, step(): pl.pallas_call(write_out, out_shape=[pltpu.HBM(o.shape, BF16) for o in ou...  7.59 us

profile of v3, /device:TPU:97, one launch (start us, length us, event | category | flops | bytes accessed | tf_op | source)
XLA Modules:
  0.0 146.3 jit_solution(6877677178369772048)
XLA Ops:
  0.6 138.1 %shard_map.102 = (bf16[2048,3072]{1,0:T(8,128)(2,1)S(1)}, bf16[3072,512]{1,0:T(8,128)(2,1)S(1)}, bf16[3072,512]{1,0:T(8,128)(2,1)S(1)}, bf16[512,3072]{1,0:T(8,128)(2,1)S(1)}) custom-call(bf16[2048,3072]{1,0:T(8,128)(2,1)} %x.1, bf16[2048,3072]{1,0:T(8,128)(2,1)} %dy.1, bf16[2048,512]{1,0:T(8,128)(2,1)} %gate.1, bf16[2048,512]{1,0:T(8,128)(2,1)} %up.1, ...), custom_call_target="tpu_custom_call" | custom-call | flops 38654705664 | bytes 62914560 | tf_op jit(solution)/shard_map/pallas_call | solution.py:334
  138.7 7.6 %shard_map.103 = (bf16[2048,3072]{1,0:T(8,128)(2,1)}, bf16[3072,512]{1,0:T(8,128)(2,1)}, bf16[3072,512]{1,0:T(8,128)(2,1)}, bf16[512,3072]{1,0:T(8,128)(2,1)}) custom-call(bf16[2048,3072]{1,0:T(8,128)(2,1)S(1)} %get-tuple-element.8.dx, bf16[3072,512]{1,0:T(8,128)(2,1)S(1)} %get-tuple-element.9.a, bf16[3072,512]{1,0:T(8,128)(2,1)S(1)} %get-tuple-element.10.b, ...), custom_call_target="tpu_custom_call" | custom-call | tf_op jit(solution)/shard_map/pallas_call | solution.py:369

commit v4 on v3

--- a/solution.py
+++ b/solution.py
@@ -11,7 +11,9 @@
 COLS = 256
 SLOTS = 4
 SIDE = 4
-ORDER = (0, 2, 1, 3)
+CUTS = 1
+EARLY = 1
+ORDER = [(j, t) for pair in ((0, 2), (1, 3)) for t in range(CUTS) for j in pair]
 NT = (((1,), (1,)), ((), ()))
 NN = (((1,), (0,)), ((), ()))
 
@@ -53,10 +55,16 @@
 
     quarters = [pl.ds(j * quarter, quarter) for j in range(4)]
 
-    def weight_quarter(j):
-        c = quarters[j]
+    cut = quarter // CUTS
+
+    def cut_at(k):
+        j, t = ORDER[k]
+        return pl.ds(j * quarter + t * cut, cut)
+
+    def weight_cut(k):
+        c = cut_at(k)
         for src, dst in ((w_gate, o_gate), (w_up, o_up)):
-            pltpu.make_async_copy(src.at[c], dst.at[c], w_sem.at[j]).start()
+            pltpu.make_async_copy(src.at[c], dst.at[c], w_sem.at[k]).start()
 
     def inputs(b):
         slot = lax.rem(b, 2)
@@ -75,6 +83,8 @@
     for j, c in enumerate(quarters):
         pltpu.make_async_copy(w_down.at[:, c], o_down.at[:, c], first_sem.at[j]).start()
         pltpu.make_async_copy(dy.at[pl.ds(0, BLOCK), c], dy_in.at[0, :, c], first_sem.at[j]).start()
+    for k in range(EARLY):
+        weight_cut(k)
 
     barrier = pltpu.get_barrier_semaphore()
     for n in x_ring + y_ring:
@@ -143,6 +153,19 @@
         for m in ms:
             for h in hs:
                 rs(b, h, m, phase).start()
+
+    def send_cut(b, h, m, t):
+        slot = lax.rem(b, SLOTS)
+        at, ring = major[h]
+        chunk = (wrap(at + 2), wrap(at + 2), wrap(at + 1), wrap(at - 1))[m]
+        c = pl.ds(t * cut, cut)
+        rows = pl.ds(pl.multiple_of(chunk * big, big), big)
+        columns = pl.ds(h * half + (0, 1, 1, 0)[m] * quarter + t * cut, cut)
+        major_send[slot, h, m, :, c] = acc[lax.rem(b, SLOTS - 1), rows, columns].astype(BF16)
+        remote(
+            major_send.at[slot, h, m, :, c], major_recv.at[slot, h, m, :, c],
+            rs_send_sem.at[slot, 0], rs_recv_sem.at[slot, 0, int(m >= 2)], ring[m % 2],
+        ).start()
 
     def scatter_second(b, phase):
         slot = lax.rem(b, SLOTS)
@@ -194,48 +217,47 @@
         silu = g * s
         return u, silu, s * (1.0 + g * (1.0 - s)), (silu * u).astype(BF16)
 
-    def term(b):
-        slot, out = lax.rem(b, 2), lax.rem(b, SLOTS - 1)
-        here = pl.ds(pl.multiple_of(b * BLOCK, BLOCK), BLOCK)
-
-        @pl.when(b == 0)
-        def _():
-            taken_rows(2 * BLOCK, first_sem.at[4])
-
-        @pl.when(b > 0)
-        def _():
-            taken_rows(BLOCK * (depth + 2 * units) // units, in_sem.at[slot])
-
+    def hidden_gradient(slot, here, ready):
         u, silu, slope, hidden = activation(slot, pl.ds(0, BLOCK))
         hidden_t[:, here] = hidden.T
         d_hidden = None
         for j, c in enumerate(quarters):
-
-            @pl.when(b == 0)
-            def _(j=j):
-                taken_rows((units + BLOCK) * quarter // units, first_sem.at[j])
-                if j == 0:
-                    for k in ORDER:
-                        weight_quarter(k)
-
+            ready(j)
             piece = dot(dy_in[slot, :, c], o_down[:, c], NT)
             d_hidden = piece if d_hidden is None else d_hidden + piece
         d_gate[here, :] = (d_hidden * u * slope).astype(BF16)
         d_up[here, :] = (d_hidden * silu).astype(BF16)
+
+    def input_gradient(out, here, c):
+        acc[out, :, c] = dot(d_gate[here, :], o_gate[c, :], NT) + dot(d_up[here, :], o_up[c, :], NT)
+
+    def first_term():
+        here = pl.ds(0, BLOCK)
+        taken_rows(2 * BLOCK, first_sem.at[4])
+
+        def ready(j):
+            taken_rows((units + BLOCK) * quarter // units, first_sem.at[j])
+            if j == 0:
+                for k in range(EARLY, 4 * CUTS):
+                    weight_cut(k)
+
+        hidden_gradient(0, here, ready)
+        inputs(1)
+        pl.semaphore_wait(barrier, 4)
+        for k, (j, t) in enumerate(ORDER):
+            taken_rows(2 * cut, w_sem.at[k])
+            input_gradient(0, here, cut_at(k))
+            for m in ((0, 3), (1, 2))[j % 2]:
+                send_cut(0, j // 2, m, t)
+
+    def term(b):
+        slot, out = lax.rem(b, 2), lax.rem(b, SLOTS - 1)
+        here = pl.ds(pl.multiple_of(b * BLOCK, BLOCK), BLOCK)
+        taken_rows(BLOCK * (depth + 2 * units) // units, in_sem.at[slot])
+        hidden_gradient(slot, here, lambda j: None)
         pl.when(b + 1 < blocks)(lambda: inputs(b + 1))
-
-        @pl.when(b == 0)
-        def _():
-            pl.semaphore_wait(barrier, 4)
-
-        for j in ORDER:
-
-            @pl.when(b == 0)
-            def _(j=j):
-                taken_rows(2 * quarter, w_sem.at[j])
-
-            cut = quarters[j]
-            acc[out, :, cut] = dot(d_gate[here, :], o_gate[cut, :], NT) + dot(d_up[here, :], o_up[cut, :], NT)
+        for j in (0, 2, 1, 3):
+            input_gradient(out, here, quarters[j])
             scatter_first(b, 0, (j // 2,), ((0, 3), (1, 2))[j % 2])
 
     def weight_gradients(k):
@@ -269,7 +291,7 @@
     def step(i, carry):
         at(i, 4, lambda b: rs_left(b, 0))
 
-        pl.when(i < blocks)(lambda: term(i))
+        pl.when(jnp.logical_and(i > 0, i < blocks))(lambda: term(i))
         pl.when(i == first_step - 1)(lambda: columns(0))
 
         def turn(b):
@@ -305,20 +327,19 @@
         at(i, 8, last)
         return carry
 
+    first_term()
     lax.fori_loop(0, blocks + 8, step, 0)
 
 
 def write_out(dx, a, b, c, o_dx, o_a, o_b, o_c, sem):
-    copies = []
-    for src, dst in ((dx, o_dx), (a, o_a), (b, o_b), (c, o_c)):
-        n = src.shape[0] // 4
-        for j in range(4):
+    pairs = ((dx, o_dx), (a, o_a), (b, o_b), (c, o_c))
+    for src, dst in pairs:
+        n = src.shape[0] // 8
+        for j in range(8):
             cut = pl.ds(j * n, n)
-            copies.append(pltpu.make_async_copy(src.at[cut], dst.at[cut], sem.at[len(copies)]))
-    for c in copies:
-        c.start()
-    for c in copies:
-        c.wait()
+            pltpu.make_async_copy(src.at[cut], dst.at[cut], sem.at[0]).start()
+    for src, dst in pairs:
+        pltpu.make_async_copy(src, dst, sem.at[0]).wait()
 
 
 def solution(mesh):
@@ -352,7 +373,7 @@
                 pltpu.VMEM((2, rows, COLS), BF16),
                 pltpu.VMEM((2, rows, COLS), BF16),
                 dma((5,)),
-                dma((4,)),
+                dma((4 * CUTS,)),
                 dma((2,)),
                 dma((2,)),
                 dma((SLOTS, 2)),
@@ -371,7 +392,7 @@
             out_shape=[pltpu.HBM(o.shape, BF16) for o in outs],
             in_specs=[pl.BlockSpec(memory_space=pltpu.VMEM)] * 4,
             out_specs=[pl.BlockSpec(memory_space=pltpu.HBM)] * 4,
-            scratch_shapes=[dma((16,))],
+            scratch_shapes=[dma((1,))],
             compiler_params=pltpu.CompilerParams(has_side_effects=True, vmem_limit_bytes=2**20),
         )(*result)
 

time: 146 us -> 146 us (level)
  no operation moved by 1% of the time
where the time goes in v4:
time: 146 us
  Pallas kernels  145 us (99%)
    pallas_call x1, Pallas kernels, step(): pl.pallas_call(kernel, out_shape=[pltpu.VMEM(o.shape, BF16) for o in outs...  138 us
    pallas_call x1, Pallas kernels, step(): pl.pallas_call(write_out, out_shape=[pltpu.HBM(o.shape, BF16) for o in ou...  7.39 us

profile of v4, /device:TPU:97, one launch (start us, length us, event | category | flops | bytes accessed | tf_op | source)
XLA Modules:
  0.0 145.7 jit_solution(708156838059757498)
XLA Ops:
  0.6 137.7 %shard_map.102 = (bf16[2048,3072]{1,0:T(8,128)(2,1)S(1)}, bf16[3072,512]{1,0:T(8,128)(2,1)S(1)}, bf16[3072,512]{1,0:T(8,128)(2,1)S(1)}, bf16[512,3072]{1,0:T(8,128)(2,1)S(1)}) custom-call(bf16[2048,3072]{1,0:T(8,128)(2,1)} %x.1, bf16[2048,3072]{1,0:T(8,128)(2,1)} %dy.1, bf16[2048,512]{1,0:T(8,128)(2,1)} %gate.1, bf16[2048,512]{1,0:T(8,128)(2,1)} %up.1, ...), custom_call_target="tpu_custom_call" | custom-call | flops 38654705664 | bytes 62914560 | tf_op jit(solution)/shard_map/pallas_call | solution.py:355
  138.3 7.4 %shard_map.103 = (bf16[2048,3072]{1,0:T(8,128)(2,1)}, bf16[3072,512]{1,0:T(8,128)(2,1)}, bf16[3072,512]{1,0:T(8,128)(2,1)}, bf16[512,3072]{1,0:T(8,128)(2,1)}) custom-call(bf16[2048,3072]{1,0:T(8,128)(2,1)S(1)} %get-tuple-element.8.dx, bf16[3072,512]{1,0:T(8,128)(2,1)S(1)} %get-tuple-element.9.a, bf16[3072,512]{1,0:T(8,128)(2,1)S(1)} %get-tuple-element.10.b, ...), custom_call_target="tpu_custom_call" | custom-call | tf_op jit(solution)/shard_map/pallas_call | solution.py:390

commit v5 on v4

--- a/solution.py
+++ b/solution.py
@@ -13,6 +13,7 @@
 SIDE = 4
 CUTS = 1
 EARLY = 1
+DEEP = 6
 ORDER = [(j, t) for pair in ((0, 2), (1, 3)) for t in range(CUTS) for j in pair]
 NT = (((1,), (1,)), ((), ()))
 NN = (((1,), (0,)), ((), ()))
@@ -54,6 +55,7 @@
         taken(d_gate.at[pl.ds(0, n)], sem)
 
     quarters = [pl.ds(j * quarter, quarter) for j in range(4)]
+    deep = [pl.ds(j * (depth // DEEP), depth // DEEP) for j in range(DEEP)]
 
     cut = quarter // CUTS
 
@@ -79,8 +81,8 @@
             pltpu.make_async_copy(src.at[:, here], dst.at[slot], cols_sem.at[slot]).start()
 
     for src, dst in ((gate, gate_in), (up, up_in)):
-        pltpu.make_async_copy(src.at[pl.ds(0, BLOCK)], dst.at[0], first_sem.at[4]).start()
-    for j, c in enumerate(quarters):
+        pltpu.make_async_copy(src.at[pl.ds(0, BLOCK)], dst.at[0], first_sem.at[DEEP]).start()
+    for j, c in enumerate(deep):
         pltpu.make_async_copy(w_down.at[:, c], o_down.at[:, c], first_sem.at[j]).start()
         pltpu.make_async_copy(dy.at[pl.ds(0, BLOCK), c], dy_in.at[0, :, c], first_sem.at[j]).start()
     for k in range(EARLY):
@@ -113,9 +115,12 @@
         slot = lax.rem(b, SLOTS)
         taken((major_send, minor_send)[phase].at[slot], rs_send_sem.at[slot, phase])
 
+    def ag_sent(b, phase):
+        return ag_send_sem.at[lax.rem(b, 3) if phase == 0 else 3 + lax.rem(b, 3)]
+
     def ag_left(b, phase):
         slot = lax.rem(b, SLOTS)
-        taken((major_send, minor_send)[phase].at[slot], ag_send_sem.at[slot, phase])
+        taken((major_send, minor_send)[phase].at[slot], ag_sent(b, phase))
 
     def ag_sem(b, h, m, phase):
         if phase == 0:
@@ -135,7 +140,7 @@
         at, ring = (major, minor)[phase][h]
         chunk = [at, at, at, at, wrap(at - 1), wrap(at + 1)][m]
         ref = place(b, h, phase, chunk, (0, 1, 1, 0, 0, 1)[m])
-        return remote(ref, ref, ag_send_sem.at[slot, phase], ag_sem(b, h, m, phase), ring[m % 2])
+        return remote(ref, ref, ag_sent(b, phase), ag_sem(b, h, m, phase), ring[m % 2])
 
     def source(b, h, phase, chunk, side):
         slot = lax.rem(b, SLOTS - 1)
@@ -221,7 +226,9 @@
         u, silu, slope, hidden = activation(slot, pl.ds(0, BLOCK))
         hidden_t[:, here] = hidden.T
         d_hidden = None
-        for j, c in enumerate(quarters):
+        if ready is None:
+            d_hidden = dot(dy_in[slot], o_down[...], NT)
+        for j, c in enumerate(deep if ready else ()):
             ready(j)
             piece = dot(dy_in[slot, :, c], o_down[:, c], NT)
             d_hidden = piece if d_hidden is None else d_hidden + piece
@@ -233,10 +240,10 @@
 
     def first_term():
         here = pl.ds(0, BLOCK)
-        taken_rows(2 * BLOCK, first_sem.at[4])
+        taken_rows(2 * BLOCK, first_sem.at[DEEP])
 
         def ready(j):
-            taken_rows((units + BLOCK) * quarter // units, first_sem.at[j])
+            taken_rows((units + BLOCK) * (depth // DEEP) // units, first_sem.at[j])
             if j == 0:
                 for k in range(EARLY, 4 * CUTS):
                     weight_cut(k)
@@ -254,7 +261,7 @@
         slot, out = lax.rem(b, 2), lax.rem(b, SLOTS - 1)
         here = pl.ds(pl.multiple_of(b * BLOCK, BLOCK), BLOCK)
         taken_rows(BLOCK * (depth + 2 * units) // units, in_sem.at[slot])
-        hidden_gradient(slot, here, lambda j: None)
+        hidden_gradient(slot, here, None)
         pl.when(b + 1 < blocks)(lambda: inputs(b + 1))
         for j in (0, 2, 1, 3):
             input_gradient(out, here, quarters[j])
@@ -306,7 +313,7 @@
             scatter_done(b, 1)
             gather_first(b, 1)
 
-        at(i, 8, lambda b: ag_left(b, 1))
+        at(i, 7, lambda b: ag_left(b, 1))
         at(i, 4, finish)
         at(i, 3, lambda b: scatter_second(b, 1))
         weights_at(i, 0)
@@ -334,8 +341,8 @@
 def write_out(dx, a, b, c, o_dx, o_a, o_b, o_c, sem):
     pairs = ((dx, o_dx), (a, o_a), (b, o_b), (c, o_c))
     for src, dst in pairs:
-        n = src.shape[0] // 8
-        for j in range(8):
+        n = src.shape[0] // 16
+        for j in range(16):
             cut = pl.ds(j * n, n)
             pltpu.make_async_copy(src.at[cut], dst.at[cut], sem.at[0]).start()
     for src, dst in pairs:
@@ -372,13 +379,13 @@
                 pltpu.VMEM((2, BLOCK, units), BF16),
                 pltpu.VMEM((2, rows, COLS), BF16),
                 pltpu.VMEM((2, rows, COLS), BF16),
-                dma((5,)),
+                dma((DEEP + 1,)),
                 dma((4 * CUTS,)),
                 dma((2,)),
                 dma((2,)),
                 dma((SLOTS, 2)),
                 dma((SLOTS, 2, 2)),
-                dma((SLOTS, 2)),
+                dma((6,)),
                 dma((SLOTS + 1, 3)),
                 dma((SLOTS, 2)),
             ],

time: 146 us -> 146 us (level)
  no operation moved by 1% of the time
where the time goes in v5:
time: 146 us
  Pallas kernels  145 us (99%)
    pallas_call x1, Pallas kernels, step(): pl.pallas_call(kernel, out_shape=[pltpu.VMEM(o.shape, BF16) for o in outs...  138 us
    pallas_call x1, Pallas kernels, step(): pl.pallas_call(write_out, out_shape=[pltpu.HBM(o.shape, BF16) for o in ou...  7.37 us

profile of v5, /device:TPU:97, one launch (start us, length us, event | category | flops | bytes accessed | tf_op | source)
XLA Modules:
  0.0 145.6 jit_solution(8080974249698088050)
XLA Ops:
  0.6 137.6 %shard_map.102 = (bf16[2048,3072]{1,0:T(8,128)(2,1)S(1)}, bf16[3072,512]{1,0:T(8,128)(2,1)S(1)}, bf16[3072,512]{1,0:T(8,128)(2,1)S(1)}, bf16[512,3072]{1,0:T(8,128)(2,1)S(1)}) custom-call(bf16[2048,3072]{1,0:T(8,128)(2,1)} %x.1, bf16[2048,3072]{1,0:T(8,128)(2,1)} %dy.1, bf16[2048,512]{1,0:T(8,128)(2,1)} %gate.1, bf16[2048,512]{1,0:T(8,128)(2,1)} %up.1, ...), custom_call_target="tpu_custom_call" | custom-call | flops 38654705664 | bytes 62914560 | tf_op jit(solution)/shard_map/pallas_call | solution.py:362
  138.3 7.4 %shard_map.103 = (bf16[2048,3072]{1,0:T(8,128)(2,1)}, bf16[3072,512]{1,0:T(8,128)(2,1)}, bf16[3072,512]{1,0:T(8,128)(2,1)}, bf16[512,3072]{1,0:T(8,128)(2,1)}) custom-call(bf16[2048,3072]{1,0:T(8,128)(2,1)S(1)} %get-tuple-element.8.dx, bf16[3072,512]{1,0:T(8,128)(2,1)S(1)} %get-tuple-element.9.a, bf16[3072,512]{1,0:T(8,128)(2,1)S(1)} %get-tuple-element.10.b, ...), custom_call_target="tpu_custom_call" | custom-call | tf_op jit(solution)/shard_map/pallas_call | solution.py:397

commit v6 on v5

--- a/solution.py
+++ b/solution.py
@@ -249,13 +249,14 @@
                     weight_cut(k)
 
         hidden_gradient(0, here, ready)
-        inputs(1)
         pl.semaphore_wait(barrier, 4)
         for k, (j, t) in enumerate(ORDER):
             taken_rows(2 * cut, w_sem.at[k])
             input_gradient(0, here, cut_at(k))
             for m in ((0, 3), (1, 2))[j % 2]:
                 send_cut(0, j // 2, m, t)
+            if k == 1:
+                inputs(1)
 
     def term(b):
         slot, out = lax.rem(b, 2), lax.rem(b, SLOTS - 1)

time: 146 us -> 146 us (level)
  no operation moved by 1% of the time
where the time goes in v6:
time: 146 us
  Pallas kernels  145 us (99%)
    pallas_call x1, Pallas kernels, step(): pl.pallas_call(kernel, out_shape=[pltpu.VMEM(o.shape, BF16) for o in outs...  138 us
    pallas_call x1, Pallas kernels, step(): pl.pallas_call(write_out, out_shape=[pltpu.HBM(o.shape, BF16) for o in ou...  7.37 us

profile of v6, /device:TPU:97, one launch (start us, length us, event | category | flops | bytes accessed | tf_op | source)
XLA Modules:
  0.0 145.7 jit_solution(6909060286557190975)
XLA Ops:
  0.6 137.6 %shard_map.102 = (bf16[2048,3072]{1,0:T(8,128)(2,1)S(1)}, bf16[3072,512]{1,0:T(8,128)(2,1)S(1)}, bf16[3072,512]{1,0:T(8,128)(2,1)S(1)}, bf16[512,3072]{1,0:T(8,128)(2,1)S(1)}) custom-call(bf16[2048,3072]{1,0:T(8,128)(2,1)} %x.1, bf16[2048,3072]{1,0:T(8,128)(2,1)} %dy.1, bf16[2048,512]{1,0:T(8,128)(2,1)} %gate.1, bf16[2048,512]{1,0:T(8,128)(2,1)} %up.1, ...), custom_call_target="tpu_custom_call" | custom-call | flops 38654705664 | bytes 62914560 | tf_op jit(solution)/shard_map/pallas_call | solution.py:363
  138.3 7.4 %shard_map.103 = (bf16[2048,3072]{1,0:T(8,128)(2,1)}, bf16[3072,512]{1,0:T(8,128)(2,1)}, bf16[3072,512]{1,0:T(8,128)(2,1)}, bf16[512,3072]{1,0:T(8,128)(2,1)}) custom-call(bf16[2048,3072]{1,0:T(8,128)(2,1)S(1)} %get-tuple-element.8.dx, bf16[3072,512]{1,0:T(8,128)(2,1)S(1)} %get-tuple-element.9.a, bf16[3072,512]{1,0:T(8,128)(2,1)S(1)} %get-tuple-element.10.b, ...), custom_call_target="tpu_custom_call" | custom-call | tf_op jit(solution)/shard_map/pallas_call | solution.py:398
